TPU v7x, 32 devices: a whole 2x2x4 slice. The times are simulated.
32 devices in a mesh: seq: 4 (over y, core), exp: 8 (over z, x).
Axes of the slice: x: 2, y: 2, z: 4, core: 2. Of those that a mesh axis runs over, the one named last changes fastest.
Arguments:
- residual_stream: bfloat16 [2048, 4096], P(('seq', 'exp')), may hold values from -6 to 6
- norm_gain: float32 [4096], replicated, may hold values from 0.25 to 1.75
- expert_ids: int32 [2048, 2], P(('seq', 'exp')), may hold values from 0 to 7, all different within a row; in each aligned block of 64 rows (0 to 63, 64 to 127, ...) at most 18 rows name the same one
- gate_weights: float32 [2048, 2], P(('seq', 'exp')), may hold values from 0.2 to 1
- w_gate: bfloat16 [8, 4096, 7168], P('exp', None, 'seq'), may hold values from -0.09375 to 0.09375
- w_up: bfloat16 [8, 4096, 7168], P('exp', None, 'seq'), may hold values from -0.09375 to 0.09375
- w_down: bfloat16 [8, 7168, 4096], P('exp', 'seq'), may hold values from -0.0625 to 0.0625
Outputs:
- moe_out: bfloat16 [2048, 4096], P(('seq', 'exp'))
Inputs may be any that keep to these rules, and one draw needn't show every extreme that they name: `expert_ids`: each row names 2 different experts. In each aligned block of 64 rows (the rows of one device) no expert is named by more than 18 rows, a bound that some blocks reach.
All inputs are finite; a program needn't handle non-finite values.
Results may differ from a plain program's by a relative error of at most 0.015.
Values may be sent and summed in bfloat16 or wider, within the bound.
No kernel may reach another device: no remote copies, remote signals or barrier semaphores. Data moves between devices by JAX's collectives and lax.ppermute only.
A program may use at most 128 MiB of HBM per device.

v0:
```python
import jax
import jax.numpy as jnp
from jax import lax
from jax.sharding import PartitionSpec as P


def expert_rows(block, gate_w, up_w, down_w):
    width = block.shape[-1]
    flat_rows = block.reshape(-1, width)
    gate = jnp.dot(flat_rows, gate_w, preferred_element_type=jnp.float32)
    up = jnp.dot(flat_rows, up_w, preferred_element_type=jnp.float32)
    hidden = (jax.nn.silu(gate) * up).astype(jnp.bfloat16)
    partial_value = jnp.dot(hidden, down_w, preferred_element_type=jnp.float32)
    return partial_value.reshape(block.shape)


def per_device(residual_stream, norm_gain, expert_ids, gate_weights, w_gate, w_up, w_down):
    rows = residual_stream.shape[0]
    width = residual_stream.shape[1]
    top = expert_ids.shape[1]
    experts = lax.axis_size("exp") * w_gate.shape[0]
    capacity = 2 * rows // experts + 2
    gate_w = w_gate[0]
    up_w = w_up[0]
    down_w = w_down[0]
    stream = residual_stream.astype(jnp.float32)
    power = jnp.mean(stream * stream, axis=1, keepdims=True)
    features = (stream * lax.rsqrt(power + 1e-06) * norm_gain[None, :]).astype(jnp.bfloat16)
    flat = expert_ids.reshape(-1)
    labels = jnp.arange(experts)
    onehot = (flat[:, None] == labels[None, :]).astype(jnp.int32)
    before = jnp.cumsum(onehot, axis=0) - onehot
    slot = jnp.sum(before * onehot, axis=1)
    target = (flat * capacity + slot).reshape(rows, top)
    places = jnp.arange(experts * capacity)
    picks = target[:, :, None] == places[None, None, :]
    dispatch = jnp.sum(picks.astype(jnp.float32), axis=1).astype(jnp.bfloat16)
    buffer = jnp.einsum("tp,td->pd", dispatch, features, preferred_element_type=jnp.float32)
    buffer = buffer.astype(jnp.bfloat16).reshape(experts, capacity, width)
    received = lax.all_to_all(buffer, "exp", split_axis=0, concat_axis=0, tiled=True)
    partials = expert_rows(
        lax.all_gather(received, "seq", axis=0, tiled=True), gate_w, up_w, down_w
    )
    owned = lax.psum_scatter(
        partials.astype(jnp.bfloat16), "seq", scatter_dimension=0, tiled=True
    ).astype(jnp.float32)
    summed = lax.all_to_all(
        owned.astype(jnp.bfloat16), "exp", split_axis=0, concat_axis=0, tiled=True
    ).astype(owned.dtype)
    weight_map = jnp.sum(picks.astype(jnp.float32) * gate_weights[:, :, None], axis=1)
    combined = jnp.dot(
        weight_map, summed.reshape(experts * capacity, width), precision=lax.Precision.HIGHEST
    )
    return combined.astype(jnp.bfloat16)


def solution(mesh):
    in_specs = (
        P(("seq", "exp"), None),
        P(),
        P(("seq", "exp"), None),
        P(("seq", "exp"), None),
        P("exp", None, "seq"),
        P("exp", None, "seq"),
        P("exp", "seq", None),
    )
    out_specs = P(("seq", "exp"), None)
    return jax.shard_map(
        per_device, mesh=mesh, in_specs=in_specs, out_specs=out_specs, check_vma=False
    )
```

profile of v0, /device:TPU:0, one launch (start us, length us, event | category | flops | bytes accessed | tf_op | source)
XLA Modules:
  0.0 255.2 jit_solution(2703196556930863798)
XLA Ops:
  6.5 1.2 fusion.15
  7.8 0.8 copy.35
  8.8 0.2 reduce_window_sum.11
  9.0 0.2 select_reduce_fusion.1
  9.2 0.1 reduce_sum.39
  9.4 0.7 multiply_add_fusion
  10.1 0.8 convert_reduce_fusion
  10.9 1.6 convolution_convert_fusion
  12.5 0.4 reshape.29
  12.9 44.1 %all_to_all.10 = bf16[8,18,4096]{2,1,0:T(8,128)(2,1)S(1)} all-to-all(bf16[8,18,4096]{2,1,0:T(8,128)(2,1)S(1)} %reshape.29), channel_id=1, replica_groups=mesh['seq'=4,'exp'=8] {'exp'}, dimensions={0} | all-to-all | bytes 2359296 | tf_op jit(solution)/shard_map/all_to_all | solution.py:40
  57.0 1.7 copy.37
  58.7 36.6 %all-gather.2.cloned.1.call-done = bf16[32,18,4096]{2,0,1:T(8,128)(2,1)} async-done(((bf16[8,18,4096]{2,0,1:T(8,128)(2,1)}), bf16[32,18,4096]{2,0,1:T(8,128)(2,1)}) %all-gather.2.cloned.1.call-update) | async-done | bytes 4718608 | tf_op jit(solution)/shard_map/all_gather | solution.py:42
  95.3 7.7 %copy.38 = bf16[32,18,4096]{2,1,0:T(8,128)(2,1)} copy(bf16[32,18,4096]{2,0,1:T(8,128)(2,1)} %all-gather.2.cloned.1.call-done) | data formatting | bytes 9437184 | tf_op jit(solution)/shard_map/all_gather | solution.py:42
  103.0 7.9 %reshape.30 = bf16[576,4096]{1,0:T(8,128)(2,1)} reshape(bf16[32,18,4096]{2,1,0:T(8,128)(2,1)} %copy.38) | data formatting | bytes 9437184 | tf_op jit(solution)/shard_map/reshape | solution.py:9
  111.0 14.7 %fusion.4 = f32[576,1792]{1,0:T(8,128)} fusion(bf16[576,4096]{1,0:T(8,128)(2,1)} %reshape.30, bf16[1,4096,1792]{2,1,0:T(8,128)(2,1)} %param.11), kind=kOutput, calls=%fused_computation.4 | convolution fusion | flops 8455716864 | bytes 23527424 | tf_op jit(solution)/shard_map/dot_general | solution.py:10
  125.7 11.6 %multiply_convert_fusion = bf16[576,1792]{1,0:T(8,128)(2,1)} fusion(f32[576,1792]{1,0:T(8,128)} %fusion.4, bf16[576,4096]{1,0:T(8,128)(2,1)S(1)} %copy-done, bf16[1,4096,1792]{2,1,0:T(8,128)(2,1)S(1)} %bitcast.29), kind=kOutput, calls=%fused_computation.10 | convolution fusion | flops 8461910016 | bytes 25591808 | tf_op jit(solution)/shard_map/dot_general | solution.py:11
  137.3 2.6 %dot_general.20 = bf16[32,18,1792]{2,1,0:T(8,128)(2,1)S(1)} reshape(bf16[576,1792]{1,0:T(8,128)(2,1)} %multiply_convert_fusion) | data formatting | bytes 4128768 | tf_op jit(solution)/shard_map/dot_general | solution.py:13
  139.9 12.0 %fusion.9 = bf16[18,4,8,4096]{3,2,1,0:T(8,128)(2,1)S(1)} fusion(bf16[1,1792,4096]{2,1,0:T(8,128)(2,1)} %param.13, bf16[32,18,1792]{2,1,0:T(8,128)(2,1)S(1)} %dot_general.20), kind=kOutput, calls=%fused_computation.7 | convolution fusion | flops 8458076160 | bytes 21463040 | tf_op jit(solution)/shard_map/dot_general | solution.py:13
  151.9 2.4 copy.43
  154.3 48.1 %reduce-scatter.4.cloned.1.call-done = bf16[8,73728]{1,0:T(8,128)(2,1)} async-done(((bf16[32,73728]{1,0:T(8,128)(2,1)}), bf16[8,73728]{1,0:T(8,128)(2,1)}) %reduce-scatter.4.cloned.1.call-update) | async-done | bytes 1179664
  202.5 2.0 copy.40
  204.4 42.1 %all_to_all.11 = bf16[8,18,4096]{2,1,0:T(8,128)(2,1)S(1)} all-to-all(bf16[8,18,4096]{2,1,0:T(8,128)(2,1)S(1)} %copy.40), channel_id=1, replica_groups=mesh['seq'=4,'exp'=8] {'exp'}, dimensions={0} | all-to-all | bytes 2359296 | tf_op jit(solution)/shard_map/all_to_all | solution.py:47
  246.6 0.4 reshape.31
  247.0 1.4 convolution_convert_fusion.1
  (19 shorter events, 0.4 us)
Async XLA Ops:
  6.5 88.7 %all-gather.2.cloned.1.call-start = ((), (), s32[]{:S(2)}) async-start(), calls=%async_computation.3 | async-start | bytes 5898240 | tf_op jit(solution)/shard_map/all_gather | solution.py:42
  58.6 143.8 %reduce-scatter.4.cloned.1.call-start = ((), (), s32[]{:S(2)}) async-start(), calls=%async_computation.4 | async-start | bytes 5898240
  103.0 22.7 %slice-start = ((s8[14680064]{0:T(1024)(128)(4,1)}), s8[2097152]{0:T(1024)(128)(4,1)S(1)}, s32[]{:S(2)}) async-start(s8[14680064]{0:T(1024)(128)(4,1)} %bitcast.28), calls=%async_computation.5 | async-start | bytes 4194304
  110.9 14.8 %copy-start = (bf16[576,4096]{1,0:T(8,128)(2,1)S(1)}, bf16[576,4096]{1,0:T(8,128)(2,1)}, u32[]{:S(2)}) copy-start(bf16[576,4096]{1,0:T(8,128)(2,1)} %reshape.30) | copy-start | bytes 14155780
  110.9 14.8 %slice-start.1 = ((s8[14680064]{0:T(1024)(128)(4,1)}), s8[4194304]{0:T(1024)(128)(4,1)S(1)}, s32[]{:S(2)}) async-start(s8[14680064]{0:T(1024)(128)(4,1)} %bitcast.28), calls=%async_computation.6 | async-start | bytes 8388608
  110.9 14.8 %slice-start.2 = ((s8[14680064]{0:T(1024)(128)(4,1)}), s8[4194304]{0:T(1024)(128)(4,1)S(1)}, s32[]{:S(2)}) async-start(s8[14680064]{0:T(1024)(128)(4,1)} %bitcast.28), calls=%async_computation.7 | async-start | bytes 8388608
  110.9 14.8 %slice-start.3 = ((s8[14680064]{0:T(1024)(128)(4,1)}), s8[4194304]{0:T(1024)(128)(4,1)S(1)}, s32[]{:S(2)}) async-start(s8[14680064]{0:T(1024)(128)(4,1)} %bitcast.28), calls=%async_computation.8 | async-start | bytes 8388608
Sparse Core Ops, SparseCore 0:
  58.8 36.4 all-gather.1
  154.5 47.9 reduce-scatter.3
where the time goes:
time: 256 us; the launch traced here: 255 us
  blocking collectives  86.2 us (34%)
  waiting for transfers between devices  84.7 us (33%)
  matrix products  41.3 us (16%)
  local copies, waits for them, and re-layouts  26.3 us (10%)
  between operations  13.5 us (5%)
  other arithmetic  3.17 us (1%)
    unnamed x3, waiting for transfers between devices  48.2 us
    all_to_all x1, blocking collectives, per_device(): lax.all_to_all(buffer, 'exp', split_axis=0, concat_axis=0, tiled=True)  44.1 us
    all_to_all x1, blocking collectives, per_device(): lax.all_to_all(owned.astype(jnp.bfloat16), 'exp', split_axis=0, concat_ax...  42.1 us
    all_gather x1, waiting for transfers between devices, per_device(): lax.all_gather(received, 'seq', axis=0, tiled=True)  36.6 us
    dot_general x1, matrix products, expert_rows(): gate = jnp.dot(flat_rows, gate_w, preferred_element_type=jnp.float32)  14.7 us
    dot_general x1, matrix products, expert_rows(): partial_value = jnp.dot(hidden, down_w, preferred_element_type=jnp.float32)  12 us
    dot_general x1, matrix products, expert_rows(): up = jnp.dot(flat_rows, up_w, preferred_element_type=jnp.float32)  11.6 us
    reshape x1, local copies, waits for them, and re-layouts, expert_rows(): flat_rows = block.reshape(-1, width)  7.94 us
  transfers between devices with their start and end apart: 2, of which 2 were waited for; matrix products, arithmetic and copies ran while one was open for 0% of the time, Pallas kernels for 0%

commit v1 on v0

v1 whole, which is shorter than its diff:
```python
import functools
import jax
import jax.numpy as jnp
from jax import lax
from jax.experimental import pallas as pl
from jax.experimental.pallas import tpu as pltpu
from jax.sharding import PartitionSpec as P

F32 = jnp.float32
BF16 = jnp.bfloat16


def iota(shape, dim):
    return lax.broadcasted_iota(jnp.int32, shape, dim)


def routes_by_row(meta, me, core, main, count):
    tokens = meta.shape[1]
    shape = (count * main, tokens)
    expert = jnp.bitwise_xor(me, 2 * (iota(shape, 0) // main) + core).astype(F32)
    named = jnp.where((meta[0:1] == expert) | (meta[1:2] == expert), 1.0, 0.0)
    earlier = jnp.where(iota((tokens, tokens), 0) < iota((tokens, tokens), 1), 1.0, 0.0)
    rank = jnp.dot(named.astype(BF16), earlier.astype(BF16), preferred_element_type=F32)
    return jnp.where(named > 0, rank, -1.0)


def routes_by_token(meta, me, core, main, count):
    tokens = meta.shape[0]
    shape = (tokens, count * main)
    expert = jnp.bitwise_xor(me, 2 * (iota(shape, 1) // main) + core).astype(F32)
    first, second = meta[:, 0:1] == expert, meta[:, 1:2] == expert
    named = jnp.where(first | second, 1.0, 0.0)
    earlier = jnp.where(iota((tokens, tokens), 1) < iota((tokens, tokens), 0), 1.0, 0.0)
    rank = jnp.dot(earlier.astype(BF16), named.astype(BF16), preferred_element_type=F32)
    weight = jnp.where(first, meta[:, 2:3], jnp.where(second, meta[:, 3:4], 0.0))
    return jnp.where(named > 0, rank, -1.0), weight


def dispatch_kernel(count, main, extra, place, own, other, own_meta, other_meta, gain, *outs):
    me, core = place[0], place[1]
    width = own.shape[1]
    ext = extra * width // main
    for half, (stream_ref, meta) in enumerate(((own, own_meta), (other, other_meta))):
        stream = stream_ref[...].astype(F32)
        power = jnp.mean(stream * stream, axis=1, keepdims=True)
        features = (stream * lax.rsqrt(power + 1e-06) * gain[...]).astype(BF16)
        rank = routes_by_row(meta[...], me, core, main, count)
        line = iota(rank.shape, 0) % main
        pick = jnp.where(rank == line.astype(F32), 1.0, 0.0).astype(BF16)
        rows = jnp.dot(pick, features, preferred_element_type=F32).astype(BF16)
        past = rank == (main + line % extra).astype(F32)
        tail = None
        for piece in range(main // extra):
            pick = jnp.where(past & (line // extra == piece), 1.0, 0.0).astype(BF16)
            part = jnp.dot(
                pick, features[:, piece * ext : (piece + 1) * ext], preferred_element_type=F32
            )
            tail = part if tail is None else tail + part
        tail = tail.astype(BF16)
        for j in range(count):
            outs[j][half * main : (half + 1) * main, 0:width] = rows[j * main : (j + 1) * main]
            outs[j][half * main : (half + 1) * main, width:] = tail[j * main : (j + 1) * main]


def combine_kernel(count, main, extra, place, own_meta, other_meta, *refs):
    blocks, (own, other) = refs[:count], refs[count:]
    me, core = place[0], place[1]
    width = own.shape[1]
    ext = extra * width // main
    for half, (meta, out) in enumerate(((own_meta, own), (other_meta, other))):
        rank, weight = routes_by_token(meta[...], me, core, main, count)
        line = iota(rank.shape, 1) % main
        cut = [b[half * main : (half + 1) * main, :] for b in blocks]
        rows = jnp.concatenate([c[:, :width] for c in cut], axis=0)
        tail = jnp.concatenate([c[:, width:] for c in cut], axis=0)

        def product(weights, values):
            high = weights.astype(BF16)
            rest = weights - high.astype(F32)
            mid = rest.astype(BF16)
            low = (rest - mid.astype(F32)).astype(BF16)
            total = jnp.dot(high, values, preferred_element_type=F32)
            total += jnp.dot(mid, values, preferred_element_type=F32)
            return total + jnp.dot(low, values, preferred_element_type=F32)

        here = jnp.where(rank == line.astype(F32), weight, 0.0)
        past = rank == (main + line % extra).astype(F32)
        for piece in range(main // extra):
            span = slice(piece * ext, (piece + 1) * ext)
            late = jnp.where(past & (line // extra == piece), weight, 0.0)
            value = product(here, rows[:, span]) + product(late, tail)
            out[:, span] = value.astype(out.dtype)


def selector(shape, match):
    return jnp.where(match(iota(shape, 0), iota(shape, 1)), 1.0, 0.0).astype(BF16)


def ffn_kernel(count, groups, main, extra, ups, downs, *refs):
    blocks, (gate_w, up_w, down_w) = refs[:count], refs[count : count + 3]
    outs = refs[count + 3 : count + 3 + groups]
    table, ext_in, hidden, ext_out, sems = refs[count + 3 + groups :]
    step = pl.program_id(0)
    rows = ext_in.shape[0]
    height = rows // count
    past = table.shape[0] - rows
    width = table.shape[1]
    ext = ext_in.shape[1]
    wide = gate_w.shape[-1]
    per = rows // groups

    @pl.when(step == 0)
    def _():
        copies = []
        for q in range(count):
            spot = pl.ds(q * height, height)
            copies.append(
                pltpu.make_async_copy(
                    blocks[q].at[:, pl.ds(0, width)], table.at[spot, :], sems.at[0, q]
                )
            )
            copies.append(
                pltpu.make_async_copy(
                    blocks[q].at[:, pl.ds(width, ext)], ext_in.at[spot, :], sems.at[1, q]
                )
            )
        for c in copies:
            c.start()
        for c in copies:
            c.wait()
        for piece in range(width // ext):
            pick = selector(
                (past, rows),
                lambda r, c: c == (r // extra) * main + extra * piece + r % extra,
            )
            table[pl.ds(rows, past), pl.ds(piece * ext, ext)] = jnp.dot(
                pick, ext_in[...], preferred_element_type=F32
            ).astype(BF16)
        ext_out[...] = jnp.zeros_like(ext_out)

    @pl.when(step < ups)
    def _():
        x = table[...]
        gate = jnp.dot(x, gate_w[...], preferred_element_type=F32)
        up = jnp.dot(x, up_w[...], preferred_element_type=F32)
        value = (gate / (1.0 + jnp.exp(-gate)) * up).astype(BF16)
        hidden[:, pl.ds(pl.multiple_of(step * wide, wide), wide)] = value

    @pl.when((step >= ups) & (step < ups + downs))
    def _():
        piece = step - ups
        partial = jnp.dot(hidden[...], down_w[...], preferred_element_type=F32).astype(BF16)
        for q in range(groups):
            outs[q][...] = partial[q * per : (q + 1) * per]
        pick = selector(
            (rows, past), lambda r, c: r == (c // extra) * main + extra * piece + c % extra
        )
        ext_out[...] += jnp.dot(pick, partial[rows:], preferred_element_type=F32)

    @pl.when(step == ups + downs)
    def _():
        value = ext_out[...].astype(BF16)
        for q in range(groups):
            outs[q][...] = value[q * per : (q + 1) * per]


def ffn(blocks, gate_w, up_w, down_w, main, extra, groups, wide=256):
    count, height = len(blocks), blocks[0].shape[0]
    width, ff = gate_w.shape
    ext = extra * width // main
    rows = count * height
    past = rows // main * extra
    ups, downs = ff // wide, width // ext
    up_spec = pl.BlockSpec((width, wide), lambda i: (0, jnp.minimum(i, ups - 1)))
    return pl.pallas_call(
        functools.partial(ffn_kernel, count, groups, main, extra, ups, downs),
        grid=(ups + downs + 1,),
        in_specs=[pl.BlockSpec(memory_space=pltpu.HBM)] * count
        + [
            up_spec,
            up_spec,
            pl.BlockSpec((ff, ext), lambda i: (0, jnp.clip(i - ups, 0, downs - 1))),
        ],
        out_specs=[
            pl.BlockSpec((rows // groups, ext), lambda i: (0, jnp.clip(i - ups, 0, downs)))
        ]
        * groups,
        out_shape=[jax.ShapeDtypeStruct((rows // groups, width + ext), BF16)] * groups,
        scratch_shapes=[
            pltpu.VMEM((rows + past, width), BF16),
            pltpu.VMEM((rows, ext), BF16),
            pltpu.VMEM((rows + past, ff), BF16),
            pltpu.VMEM((rows, ext), F32),
            pltpu.SemaphoreType.DMA((2, count)),
        ],
        cost_estimate=pl.CostEstimate(
            flops=6 * (rows + past) * width * ff,
            bytes_accessed=6 * width * ff + 4 * rows * (width + ext),
            transcendentals=(rows + past) * ff,
        ),
        compiler_params=pltpu.CompilerParams(vmem_limit_bytes=60 * 1024 * 1024),
        name="ffn",
    )(*blocks, gate_w, up_w, down_w)


def per_device(residual_stream, norm_gain, expert_ids, gate_weights, w_gate, w_up, w_down):
    tokens, width = residual_stream.shape
    top = expert_ids.shape[1]
    n_exp, n_seq = lax.axis_size("exp"), lax.axis_size("seq")
    experts = n_exp * w_gate.shape[0]
    main, extra = top * tokens // experts, 2
    ext = extra * width // main
    pairs, sides = n_exp // 2, n_seq // 2
    me, core = lax.axis_index("exp"), lax.axis_index("seq") % 2
    place = jnp.stack([me, core]).astype(jnp.int32)

    def over_seq(value, flip):
        return lax.ppermute(value, "seq", [(s, s ^ flip) for s in range(n_seq)])

    def over_exp(value, j):
        return lax.ppermute(
            value,
            ("seq", "exp"),
            [
                (s * n_exp + e, s * n_exp + (e ^ (2 * j + s % 2)))
                for s in range(n_seq)
                for e in range(n_exp)
            ],
        )

    meta = jnp.concatenate([expert_ids.astype(F32), gate_weights], axis=1)
    other = over_seq(residual_stream, 1)
    other_meta = over_seq(meta, 1)

    vmem = pl.BlockSpec(memory_space=pltpu.VMEM)
    smem = pl.BlockSpec(memory_space=pltpu.SMEM)
    blocks = pl.pallas_call(
        functools.partial(dispatch_kernel, pairs, main, extra),
        in_specs=[smem] + [vmem] * 5,
        out_specs=[vmem] * pairs,
        out_shape=[jax.ShapeDtypeStruct((2 * main, width + ext), BF16)] * pairs,
        compiler_params=pltpu.CompilerParams(vmem_limit_bytes=40 << 20),
        name="dispatch",
    )(place, residual_stream, other, meta.T, other_meta.T, norm_gain[None, :])

    order = list(range(pairs - 1, -1, -1))
    came = {j: over_exp(blocks[j], j) for j in order}
    held = []
    near, far = {}, {}
    for j in range(pairs):
        near[j] = [came[j]] + [over_seq(came[j], 2 * m) for m in range(1, sides)]
        far[j] = [over_seq(v, 1) for v in near[j]]
    for group in (near, far):
        for j in range(pairs):
            held += group[j]
    outs = ffn(held, w_gate[0], w_up[0], w_down[0], main, extra, 2 * pairs)

    height = 2 * main
    final = {}
    for j in order:
        kept, sent = outs[j], outs[pairs + j]
        total = kept.astype(F32) + over_seq(sent, 1).astype(F32)
        own = total[:height]
        for m in range(1, sides):
            own = own + over_seq(
                total[m * height : (m + 1) * height].astype(BF16), 2 * m
            ).astype(F32)
        final[j] = over_exp(own.astype(BF16), j)

    mine, theirs = pl.pallas_call(
        functools.partial(combine_kernel, pairs, main, extra),
        in_specs=[smem] + [vmem] * (2 + pairs),
        out_specs=[vmem] * 2,
        out_shape=[
            jax.ShapeDtypeStruct((tokens, width), F32),
            jax.ShapeDtypeStruct((tokens, width), BF16),
        ],
        compiler_params=pltpu.CompilerParams(vmem_limit_bytes=40 << 20),
        name="combine",
    )(place, meta, other_meta, *[final[j] for j in range(pairs)])
    return (mine + over_seq(theirs, 1).astype(F32)).astype(BF16)


def solution(mesh):
    in_specs = (
        P(("seq", "exp"), None),
        P(),
        P(("seq", "exp"), None),
        P(("seq", "exp"), None),
        P("exp", None, "seq"),
        P("exp", None, "seq"),
        P("exp", "seq", None),
    )
    out_specs = P(("seq", "exp"), None)
    return jax.shard_map(
        per_device, mesh=mesh, in_specs=in_specs, out_specs=out_specs, check_vma=False
    )
```

time: 256 us -> 155 us (0.61)
  the two profiles are of different devices: /device:TPU:0 before, /device:TPU:21 now
where the time goes in v1:
time: 155 us; the launch traced here: 154 us
  waiting for transfers between devices  77.8 us (50%)
  Pallas kernels  43.7 us (28%)
  starting transfers between devices  25.4 us (16%)
  other arithmetic  4.18 us (3%)
  local copies, waits for them, and re-layouts  2.84 us (2%)
    ppermute x8, waiting for transfers between devices, over_exp(): lax.ppermute(value, ('seq', 'exp'), [(s * n_exp + e, s * n_exp + (e ^ 2 *...  43.4 us
    pallas_call x1, Pallas kernels, ffn(): pl.pallas_call(functools.partial(ffn_kernel, count, groups, main, extra,...  39.4 us
    ppermute x23, waiting for transfers between devices, over_seq(): return lax.ppermute(value, 'seq', [(s, s ^ flip) for s in range(n_seq)])  34.4 us
    ppermute x23, starting transfers between devices, over_seq(): return lax.ppermute(value, 'seq', [(s, s ^ flip) for s in range(n_seq)])  15.5 us
    ppermute x8, starting transfers between devices, over_exp(): lax.ppermute(value, ('seq', 'exp'), [(s * n_exp + e, s * n_exp + (e ^ 2 *...  9.98 us
  transfers between devices with their start and end apart: 31, of which 16 were waited for; matrix products, arithmetic and copies ran while one was open for 2% of the time, Pallas kernels for 0%

profile of v1, /device:TPU:21, one launch (start us, length us, event | category | flops | bytes accessed | tf_op | source)
XLA Modules:
  0.0 154.3 jit_solution(12915817545843602877)
XLA Ops:
  5.2 1.6 %dispatch.1 = (bf16[32,4608]{1,0:T(8,128)(2,1)S(1)}, bf16[32,4608]{1,0:T(8,128)(2,1)S(1)}, bf16[32,4608]{1,0:T(8,128)(2,1)S(1)}, bf16[32,4608]{1,0:T(8,128)(2,1)S(1)}) custom-call(s32[2]{0:T(128)S(1)} %pad_add_fusion.place, bf16[64,4096]{1,0:T(8,128)(2,1)S(1)} %copy-done, bf16[64,4096]{1,0:T(8,128)(2,1)S(1)} %collective-permute-done.1.other, ...), custom_call_target="tpu_custom_call" | custom-call | tf_op jit(solution)/shard_map/dispatch/pallas_call | solution.py:237
  6.9 3.1 %collective-permute-start.2 = (bf16[32,4608]{1,0:T(8,128)(2,1)S(1)}, bf16[32,4608]{1,0:T(8,128)(2,1)S(1)}, u32[]{:S(2)}, u32[]{:S(2)}) collective-permute-start(bf16[32,4608]{1,0:T(8,128)(2,1)S(1)} %get-tuple-element.19), channel_id=1, source_target_pairs={{0,0},{1,1},{2,2},{3,3},{4,4},{5,5},{6,6},{7,7},{8,9},{9,8},{10,11... | collective-permute-start | bytes 884744 | tf_op jit(solution)/shard_map/ppermute | solution.py:221
  10.0 1.3 collective-permute-start.4
  12.3 1.3 collective-permute-start.8
  13.6 2.0 %collective-permute-done.2.refs_0_ = bf16[32,4608]{1,0:T(8,128)(2,1)S(1)} collective-permute-done((bf16[32,4608]{1,0:T(8,128)(2,1)S(1)}, bf16[32,4608]{1,0:T(8,128)(2,1)S(1)}, u32[]{:S(2)}, u32[]{:S(2)}) %collective-permute-start.2) | collective-permute-done | bytes 294944 | tf_op jit(solution)/shard_map/ppermute | solution.py:221
  15.8 4.9 %collective-permute-done.4.refs_2_ = bf16[32,4608]{1,0:T(8,128)(2,1)S(1)} collective-permute-done((bf16[32,4608]{1,0:T(8,128)(2,1)S(1)}, bf16[32,4608]{1,0:T(8,128)(2,1)S(1)}, u32[]{:S(2)}, u32[]{:S(2)}) %collective-permute-start.4) | collective-permute-done | bytes 294944 | tf_op jit(solution)/shard_map/ppermute | solution.py:221
  20.7 11.1 %collective-permute-done.6.refs_4_ = bf16[32,4608]{1,0:T(8,128)(2,1)S(1)} collective-permute-done((bf16[32,4608]{1,0:T(8,128)(2,1)S(1)}, bf16[32,4608]{1,0:T(8,128)(2,1)S(1)}, u32[]{:S(2)}, u32[]{:S(2)}) %collective-permute-start.6) | collective-permute-done | bytes 294944 | tf_op jit(solution)/shard_map/ppermute | solution.py:221
  32.0 6.4 %collective-permute-done.8.refs_6_ = bf16[32,4608]{1,0:T(8,128)(2,1)S(1)} collective-permute-done((bf16[32,4608]{1,0:T(8,128)(2,1)S(1)}, bf16[32,4608]{1,0:T(8,128)(2,1)S(1)}, u32[]{:S(2)}, u32[]{:S(2)}) %collective-permute-start.8) | collective-permute-done | bytes 294944 | tf_op jit(solution)/shard_map/ppermute | solution.py:221
  41.5 5.1 %collective-permute-done.7.refs_5_ = bf16[32,4608]{1,0:T(8,128)(2,1)S(1)} collective-permute-done((bf16[32,4608]{1,0:T(8,128)(2,1)S(1)}, bf16[32,4608]{1,0:T(8,128)(2,1)S(1)}, u32[]{:S(2)}, u32[]{:S(2)}) %collective-permute-start.7) | collective-permute-done | bytes 294944 | tf_op jit(solution)/shard_map/ppermute | solution.py:218
  46.6 2.2 %collective-permute-start.15 = (bf16[32,4608]{1,0:T(8,128)(2,1)S(1)}, bf16[32,4608]{1,0:T(8,128)(2,1)S(1)}, u32[]{:S(2)}, u32[]{:S(2)}) collective-permute-start(bf16[32,4608]{1,0:T(8,128)(2,1)S(1)} %collective-permute-done.7.refs_5_), channel_id=1, source_target_pairs={{0,8},{8,0},{16,24},{24,16},{1,9},{9,1},{17,25},{25,17},{2,10},{10... | collective-permute-start | bytes 884744 | tf_op jit(solution)/shard_map/ppermute | solution.py:218
  48.8 4.1 %collective-permute-done.9.refs_7_ = bf16[32,4608]{1,0:T(8,128)(2,1)S(1)} collective-permute-done((bf16[32,4608]{1,0:T(8,128)(2,1)S(1)}, bf16[32,4608]{1,0:T(8,128)(2,1)S(1)}, u32[]{:S(2)}, u32[]{:S(2)}) %collective-permute-start.9) | collective-permute-done | bytes 294944 | tf_op jit(solution)/shard_map/ppermute | solution.py:218
  52.9 1.3 collective-permute-start.17
  56.2 39.4 %ffn.1 = (bf16[64,4608]{1,0:T(8,128)(2,1)}, bf16[64,4608]{1,0:T(8,128)(2,1)}, bf16[64,4608]{1,0:T(8,128)(2,1)}, bf16[64,4608]{1,0:T(8,128)(2,1)}, bf16[64,4608]{...) custom-call(bf16[32,4608]{1,0:T(8,128)(2,1)} %copy-done.5, ...), custom_call_target="tpu_custom_call" | custom-call | flops 25367150592 | bytes 53477376 | tf_op jit(solution)/shard_map/ffn/pallas_call | solution.py:175
  99.7 1.3 collective-permute-start.22
  103.2 4.4 %collective-permute-done.19 = bf16[32,4608]{1,0:T(8,128)(2,1)S(1)} collective-permute-done((bf16[32,4608]{1,0:T(8,128)(2,1)S(1)}, bf16[32,4608]{1,0:T(8,128)(2,1)S(1)}, u32[]{:S(2)}, u32[]{:S(2)}) %collective-permute-start.19) | collective-permute-done | bytes 294944 | tf_op jit(solution)/shard_map/ppermute | solution.py:218
  107.6 2.1 %collective-permute-start.20 = (bf16[32,4608]{1,0:T(8,128)(2,1)S(1)}, bf16[32,4608]{1,0:T(8,128)(2,1)S(1)}, u32[]{:S(2)}, u32[]{:S(2)}) collective-permute-start(bf16[32,4608]{1,0:T(8,128)(2,1)S(1)} %fusion.3), channel_id=1, source_target_pairs={{0,0},{1,1},{2,2},{3,3},{4,4},{5,5},{6,6},{7,7},{8,9},{9,8},{10,11... | collective-permute-start | bytes 884744 | tf_op jit(solution)/shard_map/ppermute | solution.py:221
  109.8 4.1 %collective-permute-done.22 = bf16[32,4608]{1,0:T(8,128)(2,1)S(1)} collective-permute-done((bf16[32,4608]{1,0:T(8,128)(2,1)S(1)}, bf16[32,4608]{1,0:T(8,128)(2,1)S(1)}, u32[]{:S(2)}, u32[]{:S(2)}) %collective-permute-start.22) | collective-permute-done | bytes 294944 | tf_op jit(solution)/shard_map/ppermute | solution.py:218
  114.7 5.5 %collective-permute-done.25 = bf16[32,4608]{1,0:T(8,128)(2,1)S(1)} collective-permute-done((bf16[32,4608]{1,0:T(8,128)(2,1)S(1)}, bf16[32,4608]{1,0:T(8,128)(2,1)S(1)}, u32[]{:S(2)}, u32[]{:S(2)}) %collective-permute-start.25) | collective-permute-done | bytes 294944 | tf_op jit(solution)/shard_map/ppermute | solution.py:218
  120.4 6.1 %collective-permute-done.28 = bf16[32,4608]{1,0:T(8,128)(2,1)S(1)} collective-permute-done((bf16[32,4608]{1,0:T(8,128)(2,1)S(1)}, bf16[32,4608]{1,0:T(8,128)(2,1)S(1)}, u32[]{:S(2)}, u32[]{:S(2)}) %collective-permute-start.28) | collective-permute-done | bytes 294944 | tf_op jit(solution)/shard_map/ppermute | solution.py:218
  126.8 11.9 %collective-permute-done.26.refs_2_ = bf16[32,4608]{1,0:T(8,128)(2,1)S(1)} collective-permute-done((bf16[32,4608]{1,0:T(8,128)(2,1)S(1)}, bf16[32,4608]{1,0:T(8,128)(2,1)S(1)}, u32[]{:S(2)}, u32[]{:S(2)}) %collective-permute-start.26) | collective-permute-done | bytes 294944 | tf_op jit(solution)/shard_map/ppermute | solution.py:221
  138.7 7.2 %collective-permute-done.29.refs_3_ = bf16[32,4608]{1,0:T(8,128)(2,1)S(1)} collective-permute-done((bf16[32,4608]{1,0:T(8,128)(2,1)S(1)}, bf16[32,4608]{1,0:T(8,128)(2,1)S(1)}, u32[]{:S(2)}, u32[]{:S(2)}) %collective-permute-start.29) | collective-permute-done | bytes 294944 | tf_op jit(solution)/shard_map/ppermute | solution.py:221
  145.8 2.7 %combine.1 = (f32[64,4096]{1,0:T(8,128)S(1)}, bf16[64,4096]{1,0:T(8,128)(2,1)S(1)}) custom-call(s32[2]{0:T(128)S(1)} %pad_add_fusion.place, f32[64,4]{1,0:T(8,128)S(1)} %copy.14.own_meta, f32[64,4]{1,0:T(8,128)S(1)} %collective-permute-done.other_meta, bf16[32,4608]{1,0:T(8,128)(2,1)S(1)} %collective-permute-done.20.refs_0_, ...), custom_call_target="tpu_custom_call" | custom-call | tf_op jit(solution)/shard_map/combine/pallas_call | solution.py:270
  148.5 3.3 %collective-permute-start.30 = (bf16[64,4096]{1,0:T(8,128)(2,1)S(1)}, bf16[64,4096]{1,0:T(8,128)(2,1)S(1)}, u32[]{:S(2)}, u32[]{:S(2)}) collective-permute-start(bf16[64,4096]{1,0:T(8,128)(2,1)S(1)} %get-tuple-element.32), channel_id=1, source_target_pairs={{0,8},{8,0},{16,24},{24,16},{1,9},{9,1},{17,25},{25,17},{2,10},{10... | collective-permute-start | bytes 1572872 | tf_op jit(solution)/shard_map/ppermute | solution.py:218
  151.8 1.5 collective-permute-done.30
  (101 shorter events, 20.0 us)
Async XLA Ops:
  6.9 8.7 %collective-permute-start.2 = (bf16[32,4608]{1,0:T(8,128)(2,1)S(1)}, bf16[32,4608]{1,0:T(8,128)(2,1)S(1)}, u32[]{:S(2)}, u32[]{:S(2)}) collective-permute-start(bf16[32,4608]{1,0:T(8,128)(2,1)S(1)} %get-tuple-element.19), channel_id=1, source_target_pairs={{0,0},{1,1},{2,2},{3,3},{4,4},{5,5},{6,6},{7,7},{8,9},{9,8},{10,11... | collective-permute-start | bytes 884744 | tf_op jit(solution)/shard_map/ppermute | solution.py:221
  10.0 10.7 %collective-permute-start.4 = (bf16[32,4608]{1,0:T(8,128)(2,1)S(1)}, bf16[32,4608]{1,0:T(8,128)(2,1)S(1)}, u32[]{:S(2)}, u32[]{:S(2)}) collective-permute-start(bf16[32,4608]{1,0:T(8,128)(2,1)S(1)} %get-tuple-element.20), channel_id=1, source_target_pairs={{0,2},{1,3},{2,0},{3,1},{4,6},{5,7},{6,4},{7,5},{8,11},{9,10},{10,... | collective-permute-start | bytes 884744 | tf_op jit(solution)/shard_map/ppermute | solution.py:221
  11.3 20.5 %collective-permute-start.6 = (bf16[32,4608]{1,0:T(8,128)(2,1)S(1)}, bf16[32,4608]{1,0:T(8,128)(2,1)S(1)}, u32[]{:S(2)}, u32[]{:S(2)}) collective-permute-start(bf16[32,4608]{1,0:T(8,128)(2,1)S(1)} %get-tuple-element.21), channel_id=1, source_target_pairs={{0,4},{1,5},{2,6},{3,7},{4,0},{5,1},{6,2},{7,3},{8,13},{9,12},{10,... | collective-permute-start | bytes 884744 | tf_op jit(solution)/shard_map/ppermute | solution.py:221
  12.3 26.1 %collective-permute-start.8 = (bf16[32,4608]{1,0:T(8,128)(2,1)S(1)}, bf16[32,4608]{1,0:T(8,128)(2,1)S(1)}, u32[]{:S(2)}, u32[]{:S(2)}) collective-permute-start(bf16[32,4608]{1,0:T(8,128)(2,1)S(1)} %get-tuple-element.22), channel_id=1, source_target_pairs={{0,6},{1,7},{2,4},{3,5},{4,2},{5,3},{6,0},{7,1},{8,15},{9,14},{10,... | collective-permute-start | bytes 884744 | tf_op jit(solution)/shard_map/ppermute | solution.py:221
  15.6 22.8 %collective-permute-start.10 = (bf16[32,4608]{1,0:T(8,128)(2,1)S(1)}, bf16[32,4608]{1,0:T(8,128)(2,1)S(1)}, u32[]{:S(2)}, u32[]{:S(2)}) collective-permute-start(bf16[32,4608]{1,0:T(8,128)(2,1)S(1)} %collective-permute-done.2.refs_0_), channel_id=1, source_target_pairs={{0,8},{8,0},{16,24},{24,16},{1,9},{9,1},{17,25},{25,17},{2,10},{10... | collective-permute-start | bytes 884744 | tf_op jit(solution)/shard_map/ppermute | solution.py:218
  15.6 23.1 %collective-permute-start.3 = (bf16[32,4608]{1,0:T(8,128)(2,1)S(1)}, bf16[32,4608]{1,0:T(8,128)(2,1)S(1)}, u32[]{:S(2)}, u32[]{:S(2)}) collective-permute-start(bf16[32,4608]{1,0:T(8,128)(2,1)S(1)} %collective-permute-done.2.refs_0_), channel_id=1, source_target_pairs={{0,16},{8,24},{16,0},{24,8},{1,17},{9,25},{17,1},{25,9},{2,18},{10... | collective-permute-start | bytes 884744 | tf_op jit(solution)/shard_map/ppermute | solution.py:218
  20.7 19.2 %collective-permute-start.12 = (bf16[32,4608]{1,0:T(8,128)(2,1)S(1)}, bf16[32,4608]{1,0:T(8,128)(2,1)S(1)}, u32[]{:S(2)}, u32[]{:S(2)}) collective-permute-start(bf16[32,4608]{1,0:T(8,128)(2,1)S(1)} %collective-permute-done.4.refs_2_), channel_id=1, source_target_pairs={{0,8},{8,0},{16,24},{24,16},{1,9},{9,1},{17,25},{25,17},{2,10},{10... | collective-permute-start | bytes 884744 | tf_op jit(solution)/shard_map/ppermute | solution.py:218
  31.8 9.2 %collective-permute-start.5 = (bf16[32,4608]{1,0:T(8,128)(2,1)S(1)}, bf16[32,4608]{1,0:T(8,128)(2,1)S(1)}, u32[]{:S(2)}, u32[]{:S(2)}) collective-permute-start(bf16[32,4608]{1,0:T(8,128)(2,1)S(1)} %collective-permute-done.4.refs_2_), channel_id=1, source_target_pairs={{0,16},{8,24},{16,0},{24,8},{1,17},{9,25},{17,1},{25,9},{2,18},{10... | collective-permute-start | bytes 884744 | tf_op jit(solution)/shard_map/ppermute | solution.py:218
  38.4 8.2 %collective-permute-start.7 = (bf16[32,4608]{1,0:T(8,128)(2,1)S(1)}, bf16[32,4608]{1,0:T(8,128)(2,1)S(1)}, u32[]{:S(2)}, u32[]{:S(2)}) collective-permute-start(bf16[32,4608]{1,0:T(8,128)(2,1)S(1)} %collective-permute-done.6.refs_4_), channel_id=1, source_target_pairs={{0,16},{8,24},{16,0},{24,8},{1,17},{9,25},{17,1},{25,9},{2,18},{10... | collective-permute-start | bytes 884744 | tf_op jit(solution)/shard_map/ppermute | solution.py:218
  38.7 14.2 %collective-permute-start.9 = (bf16[32,4608]{1,0:T(8,128)(2,1)S(1)}, bf16[32,4608]{1,0:T(8,128)(2,1)S(1)}, u32[]{:S(2)}, u32[]{:S(2)}) collective-permute-start(bf16[32,4608]{1,0:T(8,128)(2,1)S(1)} %collective-permute-done.8.refs_6_), channel_id=1, source_target_pairs={{0,16},{8,24},{16,0},{24,8},{1,17},{9,25},{17,1},{25,9},{2,18},{10... | collective-permute-start | bytes 884744 | tf_op jit(solution)/shard_map/ppermute | solution.py:218
  39.9 14.3 %collective-permute-start.16 = (bf16[32,4608]{1,0:T(8,128)(2,1)S(1)}, bf16[32,4608]{1,0:T(8,128)(2,1)S(1)}, u32[]{:S(2)}, u32[]{:S(2)}) collective-permute-start(bf16[32,4608]{1,0:T(8,128)(2,1)S(1)} %collective-permute-done.8.refs_6_), channel_id=1, source_target_pairs={{0,8},{8,0},{16,24},{24,16},{1,9},{9,1},{17,25},{25,17},{2,10},{10... | collective-permute-start | bytes 884744 | tf_op jit(solution)/shard_map/ppermute | solution.py:218
  40.9 13.3 %collective-permute-start.11 = (bf16[32,4608]{1,0:T(8,128)(2,1)S(1)}, bf16[32,4608]{1,0:T(8,128)(2,1)S(1)}, u32[]{:S(2)}, u32[]{:S(2)}) collective-permute-start(bf16[32,4608]{1,0:T(8,128)(2,1)S(1)} %collective-permute-done.3.refs_1_), channel_id=1, source_target_pairs={{0,8},{8,0},{16,24},{24,16},{1,9},{9,1},{17,25},{25,17},{2,10},{10... | collective-permute-start | bytes 884744 | tf_op jit(solution)/shard_map/ppermute | solution.py:218
  41.0 13.2 %collective-permute-start.13 = (bf16[32,4608]{1,0:T(8,128)(2,1)S(1)}, bf16[32,4608]{1,0:T(8,128)(2,1)S(1)}, u32[]{:S(2)}, u32[]{:S(2)}) collective-permute-start(bf16[32,4608]{1,0:T(8,128)(2,1)S(1)} %collective-permute-done.5.refs_3_), channel_id=1, source_target_pairs={{0,8},{8,0},{16,24},{24,16},{1,9},{9,1},{17,25},{25,17},{2,10},{10... | collective-permute-start | bytes 884744 | tf_op jit(solution)/shard_map/ppermute | solution.py:218
  46.6 7.7 %collective-permute-start.15 = (bf16[32,4608]{1,0:T(8,128)(2,1)S(1)}, bf16[32,4608]{1,0:T(8,128)(2,1)S(1)}, u32[]{:S(2)}, u32[]{:S(2)}) collective-permute-start(bf16[32,4608]{1,0:T(8,128)(2,1)S(1)} %collective-permute-done.7.refs_5_), channel_id=1, source_target_pairs={{0,8},{8,0},{16,24},{24,16},{1,9},{9,1},{17,25},{25,17},{2,10},{10... | collective-permute-start | bytes 884744 | tf_op jit(solution)/shard_map/ppermute | solution.py:218
  96.7 5.5 %collective-permute-start.27 = (bf16[64,4608]{1,0:T(8,128)(2,1)}, bf16[64,4608]{1,0:T(8,128)(2,1)S(1)}, u32[]{:S(2)}, u32[]{:S(2)}) collective-permute-start(bf16[64,4608]{1,0:T(8,128)(2,1)} %get-tuple-element.30), channel_id=1, source_target_pairs={{0,8},{8,0},{16,24},{24,16},{1,9},{9,1},{17,25},{25,17},{2,10},{10... | collective-permute-start | bytes 1769480 | tf_op jit(solution)/shard_map/ppermute | solution.py:218
  99.3 8.3 %collective-permute-start.19 = (bf16[32,4608]{1,0:T(8,128)(2,1)S(1)}, bf16[32,4608]{1,0:T(8,128)(2,1)S(1)}, u32[]{:S(2)}, u32[]{:S(2)}) collective-permute-start(bf16[32,4608]{1,0:T(8,128)(2,1)S(1)} %slice.63), channel_id=1, source_target_pairs={{0,16},{8,24},{16,0},{24,8},{1,17},{9,25},{17,1},{25,9},{2,18},{10... | collective-permute-start | bytes 884744 | tf_op jit(solution)/shard_map/ppermute | solution.py:218
  99.7 14.1 %collective-permute-start.22 = (bf16[32,4608]{1,0:T(8,128)(2,1)S(1)}, bf16[32,4608]{1,0:T(8,128)(2,1)S(1)}, u32[]{:S(2)}, u32[]{:S(2)}) collective-permute-start(bf16[32,4608]{1,0:T(8,128)(2,1)S(1)} %slice.62), channel_id=1, source_target_pairs={{0,16},{8,24},{16,0},{24,8},{1,17},{9,25},{17,1},{25,9},{2,18},{10... | collective-permute-start | bytes 884744 | tf_op jit(solution)/shard_map/ppermute | solution.py:218
  101.2 19.0 %collective-permute-start.25 = (bf16[32,4608]{1,0:T(8,128)(2,1)S(1)}, bf16[32,4608]{1,0:T(8,128)(2,1)S(1)}, u32[]{:S(2)}, u32[]{:S(2)}) collective-permute-start(bf16[32,4608]{1,0:T(8,128)(2,1)S(1)} %slice.61), channel_id=1, source_target_pairs={{0,16},{8,24},{16,0},{24,8},{1,17},{9,25},{17,1},{25,9},{2,18},{10... | collective-permute-start | bytes 884744 | tf_op jit(solution)/shard_map/ppermute | solution.py:218
  102.3 24.2 %collective-permute-start.28 = (bf16[32,4608]{1,0:T(8,128)(2,1)S(1)}, bf16[32,4608]{1,0:T(8,128)(2,1)S(1)}, u32[]{:S(2)}, u32[]{:S(2)}) collective-permute-start(bf16[32,4608]{1,0:T(8,128)(2,1)S(1)} %slice.60), channel_id=1, source_target_pairs={{0,16},{8,24},{16,0},{24,8},{1,17},{9,25},{17,1},{25,9},{2,18},{10... | collective-permute-start | bytes 884744 | tf_op jit(solution)/shard_map/ppermute | solution.py:218
  107.6 19.2 %collective-permute-start.20 = (bf16[32,4608]{1,0:T(8,128)(2,1)S(1)}, bf16[32,4608]{1,0:T(8,128)(2,1)S(1)}, u32[]{:S(2)}, u32[]{:S(2)}) collective-permute-start(bf16[32,4608]{1,0:T(8,128)(2,1)S(1)} %fusion.3), channel_id=1, source_target_pairs={{0,0},{1,1},{2,2},{3,3},{4,4},{5,5},{6,6},{7,7},{8,9},{9,8},{10,11... | collective-permute-start | bytes 884744 | tf_op jit(solution)/shard_map/ppermute | solution.py:221
  113.9 12.9 %collective-permute-start.23 = (bf16[32,4608]{1,0:T(8,128)(2,1)S(1)}, bf16[32,4608]{1,0:T(8,128)(2,1)S(1)}, u32[]{:S(2)}, u32[]{:S(2)}) collective-permute-start(bf16[32,4608]{1,0:T(8,128)(2,1)S(1)} %fusion.2), channel_id=1, source_target_pairs={{0,2},{1,3},{2,0},{3,1},{4,6},{5,7},{6,4},{7,5},{8,11},{9,10},{10,... | collective-permute-start | bytes 884744 | tf_op jit(solution)/shard_map/ppermute | solution.py:221
  120.2 18.4 %collective-permute-start.26 = (bf16[32,4608]{1,0:T(8,128)(2,1)S(1)}, bf16[32,4608]{1,0:T(8,128)(2,1)S(1)}, u32[]{:S(2)}, u32[]{:S(2)}) collective-permute-start(bf16[32,4608]{1,0:T(8,128)(2,1)S(1)} %fusion.1), channel_id=1, source_target_pairs={{0,4},{1,5},{2,6},{3,7},{4,0},{5,1},{6,2},{7,3},{8,13},{9,12},{10,... | collective-permute-start | bytes 884744 | tf_op jit(solution)/shard_map/ppermute | solution.py:221
  126.5 19.3 %collective-permute-start.29 = (bf16[32,4608]{1,0:T(8,128)(2,1)S(1)}, bf16[32,4608]{1,0:T(8,128)(2,1)S(1)}, u32[]{:S(2)}, u32[]{:S(2)}) collective-permute-start(bf16[32,4608]{1,0:T(8,128)(2,1)S(1)} %fusion), channel_id=1, source_target_pairs={{0,6},{1,7},{2,4},{3,5},{4,2},{5,3},{6,0},{7,1},{8,15},{9,14},{10,... | collective-permute-start | bytes 884744 | tf_op jit(solution)/shard_map/ppermute | solution.py:221
  148.5 4.9 %collective-permute-start.30 = (bf16[64,4096]{1,0:T(8,128)(2,1)S(1)}, bf16[64,4096]{1,0:T(8,128)(2,1)S(1)}, u32[]{:S(2)}, u32[]{:S(2)}) collective-permute-start(bf16[64,4096]{1,0:T(8,128)(2,1)S(1)} %get-tuple-element.32), channel_id=1, source_target_pairs={{0,8},{8,0},{16,24},{24,16},{1,9},{9,1},{17,25},{25,17},{2,10},{10... | collective-permute-start | bytes 1572872 | tf_op jit(solution)/shard_map/ppermute | solution.py:218
  (28 other events, 246.0 us)
